TPU v7x, 32 devices: a whole 2x2x4 slice. The times are simulated.
32 devices in a mesh: dp: 4 (over z), tensor: 8 (over y, x, core).
Axes of the slice: x: 2, y: 2, z: 4, core: 2. Of those that a mesh axis runs over, the one named last changes fastest.
Arguments:
- tokens: bfloat16 [1024, 4096], P(('dp', 'tensor')), may hold values from -4 to 4
- lengths: int32 [4], replicated, may hold values from 64 to 256, as said below
- norm_gains: float32 [2, 4096], replicated, may hold values from 0.25 to 1.75
- query_weight: bfloat16 [2, 4096, 4096], P(None, None, 'tensor'), may hold values from -0.09375 to 0.09375
- key_weight: bfloat16 [2, 4096, 1024], P(None, None, 'tensor'), may hold values from -0.09375 to 0.09375
- value_weight: bfloat16 [2, 4096, 1024], P(None, None, 'tensor'), may hold values from -0.09375 to 0.09375
- out_weight: bfloat16 [2, 4096, 4096], P(None, 'tensor'), may hold values from -0.09375 to 0.09375
- query_probe: bfloat16 [2, 4096, 4096], P(None, 'dp', 'tensor'), may hold values from -0.09375 to 0.09375
- key_probe: bfloat16 [2, 4096, 1024], P(None, 'dp', 'tensor'), may hold values from -0.09375 to 0.09375
- value_probe: bfloat16 [2, 4096, 1024], P(None, 'dp', 'tensor'), may hold values from -0.09375 to 0.09375
- out_probe: bfloat16 [2, 4096, 4096], P(None, 'tensor', 'dp'), may hold values from -0.09375 to 0.09375
Outputs:
- query_product: float32 [2, 4096, 4096], P(None, 'dp', 'tensor')
- key_product: float32 [2, 4096, 1024], P(None, 'dp', 'tensor')
- value_product: float32 [2, 4096, 1024], P(None, 'dp', 'tensor')
- out_product: float32 [2, 4096, 4096], P(None, 'tensor', 'dp')
Inputs may be any that keep to these rules, and one draw needn't show every extreme that they name: lengths[i] counts the leading valid positions of sequence i; the last sequence is full.
All inputs are finite; a program needn't handle non-finite values.
Results may differ from a plain program's by a relative error of at most 0.035.
Values may be sent and summed in bfloat16 or wider, within the bound.
A program may use at most 128 MiB of HBM per device.

v0:
```python
import math
import jax
import jax.numpy as jnp
from jax import lax
from jax.sharding import PartitionSpec as P

KVH = 8
HD = 128
LEN = 256
EPS = 1e-05
THETA = 500000.0


def swapped(value, axis, apart):
    mask = 2**apart
    pairs = [(source, source ^ mask) for source in range(lax.axis_size(axis))]
    return lax.ppermute(value, axis, pairs)


def multiply(pattern, left_side, right_side):
    return jnp.einsum(pattern, left_side, right_side, preferred_element_type=jnp.float32)


def matmul(left_side, right_side):
    return jnp.dot(left_side, right_side, preferred_element_type=jnp.float32)


def contract_rows(left_side, right_side):
    return lax.dot_general(
        left_side, right_side, (((0,), (0,)), ((), ())), preferred_element_type=jnp.float32
    )


def contract_last(left_side, right_side):
    return lax.dot_general(
        left_side, right_side, (((1,), (1,)), ((), ())), preferred_element_type=jnp.float32
    )


def rope_tables(length, head_size):
    position = jnp.arange(length).astype(jnp.float32)
    column = jnp.arange(head_size // 2).astype(jnp.float32)
    frequency = jnp.exp(-math.log(THETA) * 2.0 * column / head_size)
    angles = position[:, None] * frequency[None, :]
    return (jnp.cos(angles), jnp.sin(angles))


def rotate(values, cosine_table, sine_table, direction):
    middle = values.shape[-1] // 2
    leading = values[..., :middle]
    trailing = values[..., middle:]
    cosine = cosine_table[None, :, None, :]
    sine_part = direction * sine_table[None, :, None, :]
    return jnp.concatenate(
        [leading * cosine - trailing * sine_part, trailing * cosine + leading * sine_part], axis=-1
    )


def allowed_mask(size, length):
    row_index = jnp.arange(size)[:, None]
    column_index = jnp.arange(size)[None, :]
    return (column_index <= row_index) & (column_index < length)


def attend(queries, key_heads, value_heads, tangent_queries, tangent_keys, tangent_values, length):
    repeat = queries.shape[1] // key_heads.shape[1]
    key_heads = jnp.repeat(key_heads, repeat, axis=1)
    value_heads = jnp.repeat(value_heads, repeat, axis=1)
    tangent_keys = jnp.repeat(tangent_keys, repeat, axis=1)
    tangent_values = jnp.repeat(tangent_values, repeat, axis=1)
    scaling = 1.0 / math.sqrt(queries.shape[-1])
    allowed = allowed_mask(queries.shape[0], length)[None]
    scores = multiply("ihd,jhd->hij", queries, key_heads) * scaling
    powers = jnp.where(allowed, jnp.exp(scores), 0.0)
    weights = powers / jnp.sum(powers, axis=-1, keepdims=True)
    weights_low = weights.astype(jnp.bfloat16)
    blended = multiply("hij,jhd->ihd", weights_low, value_heads).astype(jnp.bfloat16)
    tangent_scores = (
        multiply("ihd,jhd->hij", tangent_queries, key_heads)
        + multiply("ihd,jhd->hij", queries, tangent_keys)
    ) * scaling
    tangent_weights = weights * (
        tangent_scores - jnp.sum(weights * tangent_scores, axis=-1, keepdims=True)
    )
    tangent_blended = multiply(
        "hij,jhd->ihd", tangent_weights.astype(jnp.bfloat16), value_heads
    ) + multiply("hij,jhd->ihd", weights_low, tangent_values)
    return (blended, tangent_blended.astype(jnp.bfloat16))


def attend_back(queries, key_heads, value_heads, grad_mixed, length):
    repeat = queries.shape[1] // key_heads.shape[1]
    key_heads = jnp.repeat(key_heads, repeat, axis=1)
    value_heads = jnp.repeat(value_heads, repeat, axis=1)
    scaling = 1.0 / math.sqrt(queries.shape[-1])
    allowed = allowed_mask(queries.shape[0], length)[None]
    scores = multiply("ihd,jhd->hij", queries, key_heads) * scaling
    powers = jnp.where(allowed, jnp.exp(scores), 0.0)
    weights = powers / jnp.sum(powers, axis=-1, keepdims=True)
    weights_low = weights.astype(jnp.bfloat16)
    grad_weights = multiply("ihd,jhd->hij", grad_mixed, value_heads)
    grad_values = multiply("hij,ihd->jhd", weights_low, grad_mixed)
    grad_scores = (
        weights * (grad_weights - jnp.sum(weights * grad_weights, axis=-1, keepdims=True)) * scaling
    ).astype(jnp.bfloat16)
    grad_queries = multiply("hij,jhd->ihd", grad_scores, key_heads)
    grad_keys = multiply("hij,ihd->jhd", grad_scores, queries)
    return (grad_queries, grad_keys, grad_values)


def normalize(stream, gain_row):
    wide_stream = stream.astype(jnp.float32)
    inverse = lax.rsqrt(jnp.mean(wide_stream * wide_stream, axis=-1, keepdims=True) + EPS)
    return (wide_stream, inverse, (wide_stream * inverse * gain_row).astype(jnp.bfloat16))


def norm_tangent(wide_stream, inverse, tangent, gain_row):
    shift = jnp.mean(wide_stream * tangent, axis=-1, keepdims=True)
    return (
        gain_row * (tangent * inverse - wide_stream * inverse * inverse * inverse * shift)
    ).astype(jnp.bfloat16)


def norm_back(wide_stream, inverse, grad_normed, gain_row):
    scaled = grad_normed * gain_row
    shift = jnp.mean(wide_stream * scaled, axis=-1, keepdims=True)
    return inverse * (scaled - wide_stream * inverse * inverse * shift)


def body(
    tokens,
    lengths,
    norm_gains,
    query_weight,
    key_weight,
    value_weight,
    out_weight,
    query_probe,
    key_probe,
    value_probe,
    out_probe,
):
    tensor_count = lax.axis_size("tensor")
    tensor_index = lax.axis_index("tensor")
    data_index = lax.axis_index("dp")
    share_rows = tokens.shape[0]
    group_rows = share_rows * tensor_count
    seq_count = group_rows // LEN
    layer_count = query_weight.shape[0]
    half_width = key_weight.shape[2]
    cosine_table, sine_table = rope_tables(LEN, HD)
    group_lengths = lax.dynamic_slice_in_dim(lengths, data_index * seq_count, seq_count)
    position = jnp.arange(group_rows) % LEN
    group_mask = (position < jnp.repeat(group_lengths, LEN)).astype(jnp.float32)
    lower_half = tensor_index % 2 == 0
    paired = tensor_count > KVH

    def heads_of(values):
        return values.reshape(seq_count, LEN, -1, HD)

    def join_halves(own_part, other_part):
        return jnp.where(
            lower_half,
            jnp.concatenate([own_part, other_part], axis=-1),
            jnp.concatenate([other_part, own_part], axis=-1),
        )

    def own_columns(values):
        return jnp.where(lower_half, values[:, :half_width], values[:, half_width:])

    def other_columns(values):
        return jnp.where(lower_half, values[:, half_width:], values[:, :half_width])

    query_full_probe, key_own_probe, value_own_probe, out_full_probe = (
        lax.all_gather(query_probe, "dp", axis=1, tiled=True),
        lax.all_gather(key_probe, "dp", axis=1, tiled=True),
        lax.all_gather(value_probe, "dp", axis=1, tiled=True),
        lax.all_gather(out_probe, "dp", axis=2, tiled=True),
    )
    owned_parts = (key_weight, value_weight, key_own_probe, value_own_probe)
    if paired:
        partner = swapped((key_weight, value_weight, key_own_probe, value_own_probe), "tensor", 0)
        joined = [
            join_halves(own_part, other_part) for own_part, other_part in zip(owned_parts, partner)
        ]
        key_full, value_full, key_full_probe, value_full_probe = joined
    else:
        key_full, value_full, key_full_probe, value_full_probe = owned_parts
    stream = lax.all_gather(tokens, "tensor", axis=0, tiled=True)
    tangent = None
    stored = []
    for layer_index in range(layer_count):
        final_layer = layer_index == layer_count - 1
        gain_row = norm_gains[layer_index]
        wide_stream, inverse, normed = normalize(stream, gain_row)
        tangent_normed = (
            None if tangent is None else norm_tangent(wide_stream, inverse, tangent, gain_row)
        )
        normed_all, tangent_all = (normed, tangent_normed)

        def project(weight, probe_part):
            primal = matmul(normed_all, weight)
            moved_part = matmul(normed_all, probe_part)
            if tangent_all is not None:
                moved_part = moved_part + matmul(tangent_all, weight)
            return (primal, moved_part)

        query_primal, query_moved = project(
            query_weight[layer_index], query_full_probe[layer_index]
        )
        key_primal, key_moved = project(key_full[layer_index], key_full_probe[layer_index])
        value_primal, value_moved = project(value_full[layer_index], value_full_probe[layer_index])
        queries = rotate(heads_of(query_primal), cosine_table, sine_table, 1.0).astype(jnp.bfloat16)
        key_heads = rotate(heads_of(key_primal), cosine_table, sine_table, 1.0).astype(jnp.bfloat16)
        value_heads = heads_of(value_primal).astype(jnp.bfloat16)
        tangent_queries = rotate(heads_of(query_moved), cosine_table, sine_table, 1.0).astype(
            jnp.bfloat16
        )
        tangent_keys = rotate(heads_of(key_moved), cosine_table, sine_table, 1.0).astype(
            jnp.bfloat16
        )
        tangent_values = heads_of(value_moved).astype(jnp.bfloat16)
        blended, tangent_blended = lax.map(
            lambda pieces: attend(*pieces),
            (
                queries,
                key_heads,
                value_heads,
                tangent_queries,
                tangent_keys,
                tangent_values,
                group_lengths,
            ),
        )
        blended = blended.reshape(group_rows, -1)
        tangent_blended = tangent_blended.reshape(group_rows, -1)
        tangent_part = matmul(tangent_blended, out_weight[layer_index]) + matmul(
            blended, out_full_probe[layer_index]
        )
        if final_layer:
            tangent_sum = lax.psum(tangent_part.astype(jnp.bfloat16), "tensor").astype(jnp.float32)
        else:
            primal_part = matmul(blended, out_weight[layer_index])
            primal_sum, tangent_sum = (
                lax.psum(primal_part.astype(jnp.bfloat16), "tensor").astype(jnp.float32),
                lax.psum(tangent_part.astype(jnp.bfloat16), "tensor").astype(jnp.float32),
            )
        stored.append((wide_stream, inverse, normed_all, queries, key_heads, value_heads, blended))
        if not final_layer:
            stream = (wide_stream + primal_sum).astype(jnp.bfloat16)
        tangent = tangent_sum if tangent is None else tangent + tangent_sum
    cotangent = group_mask[:, None] * tangent
    collected = [None] * layer_count
    for layer_index in reversed(range(layer_count)):
        wide_stream, inverse, normed_all, queries, key_heads, value_heads, blended = stored[
            layer_index
        ]
        cotangent_low = cotangent.astype(jnp.bfloat16)
        out_product = contract_rows(blended, cotangent_low)
        grad_mixed = contract_last(cotangent_low, out_weight[layer_index]).astype(jnp.bfloat16)
        grad_queries, grad_keys, grad_values = lax.map(
            lambda pieces: attend_back(*pieces),
            (queries, key_heads, value_heads, heads_of(grad_mixed), group_lengths),
        )
        key_count = key_heads.shape[2]
        query_low = (
            rotate(grad_queries, cosine_table, sine_table, -1.0)
            .astype(jnp.bfloat16)
            .reshape(group_rows, -1)
        )
        key_grouped = grad_keys.reshape(seq_count, LEN, key_count, -1, HD).sum(axis=3)
        key_low = (
            rotate(key_grouped, cosine_table, sine_table, -1.0)
            .astype(jnp.bfloat16)
            .reshape(group_rows, -1)
        )
        value_low = (
            grad_values.reshape(seq_count, LEN, key_count, -1, HD)
            .sum(axis=3)
            .astype(jnp.bfloat16)
            .reshape(group_rows, -1)
        )
        query_product = contract_rows(normed_all, query_low)
        key_product = contract_rows(normed_all, key_low)
        value_product = contract_rows(normed_all, value_low)
        if paired:
            key_back, value_back = (
                swapped(other_columns(key_product).astype(jnp.bfloat16), "tensor", 0).astype(
                    jnp.float32
                ),
                swapped(other_columns(value_product).astype(jnp.bfloat16), "tensor", 0).astype(
                    jnp.float32
                ),
            )
            key_product = own_columns(key_product) + key_back
            value_product = own_columns(value_product) + value_back
        collected[layer_index] = (query_product, key_product, value_product, out_product)
        if layer_index > 0:
            grad_part = contract_last(query_low, query_weight[layer_index])
            grad_part = (
                grad_part
                + contract_last(key_low, key_full[layer_index])
                + contract_last(value_low, value_full[layer_index])
            )
            grad_normed = lax.psum(grad_part.astype(jnp.bfloat16), "tensor").astype(jnp.float32)
            cotangent = cotangent + norm_back(
                wide_stream, inverse, grad_normed, norm_gains[layer_index]
            )
    query_stack = jnp.stack([collected[number][0] for number in range(layer_count)])
    key_stack = jnp.stack([collected[number][1] for number in range(layer_count)])
    value_stack = jnp.stack([collected[number][2] for number in range(layer_count)])
    out_stack = jnp.stack([collected[number][3] for number in range(layer_count)])
    query_stack, key_stack, value_stack, out_stack = (
        lax.psum_scatter(
            query_stack.astype(jnp.bfloat16), "dp", scatter_dimension=1, tiled=True
        ).astype(jnp.float32),
        lax.psum_scatter(
            key_stack.astype(jnp.bfloat16), "dp", scatter_dimension=1, tiled=True
        ).astype(jnp.float32),
        lax.psum_scatter(
            value_stack.astype(jnp.bfloat16), "dp", scatter_dimension=1, tiled=True
        ).astype(jnp.float32),
        lax.psum_scatter(
            out_stack.astype(jnp.bfloat16), "dp", scatter_dimension=2, tiled=True
        ).astype(jnp.float32),
    )
    return (query_stack, key_stack, value_stack, out_stack)


def solution(mesh):
    placed = (
        P(("dp", "tensor"), None),
        P(),
        P(),
        P(None, None, "tensor"),
        P(None, None, "tensor"),
        P(None, None, "tensor"),
        P(None, "tensor", None),
        P(None, "dp", "tensor"),
        P(None, "dp", "tensor"),
        P(None, "dp", "tensor"),
        P(None, "tensor", "dp"),
    )
    return jax.shard_map(
        body,
        mesh=mesh,
        in_specs=placed,
        out_specs=(
            P(None, "dp", "tensor"),
            P(None, "dp", "tensor"),
            P(None, "dp", "tensor"),
            P(None, "tensor", "dp"),
        ),
        check_vma=False,
    )
```

profile of v0, /device:TPU:0, one launch (start us, length us, event | category | flops | bytes accessed | tf_op | source)
XLA Modules:
  0.0 1128.5 jit_solution(12675295686108576268)
XLA Ops:
  10.6 5.8 slice_bitcast_fusion.8
  16.4 6.3 copy.15
  25.1 15.2 %all-gather.6.cloned.1.call-done = bf16[256,4096]{1,0:T(8,128)(2,1)} async-done(((bf16[32,4096]{1,0:T(8,128)(2,1)}), bf16[256,4096]{1,0:T(8,128)(2,1)}) %all-gather.6.cloned.1.call-update) | async-done | bytes 2097168 | tf_op jit(solution)/shard_map/all_gather | solution.py:189
  40.4 2.1 fusion.26
  42.5 2.2 fusion.28
  44.7 2.8 convolution_bitcast_fusion.8
  47.5 40.2 %all-gather.10.cloned.1.call-done = bf16[2,4096,128]{2,1,0:T(8,128)(2,1)} async-done(((bf16[2,1024,128]{2,1,0:T(8,128)(2,1)}), bf16[2,4096,128]{2,1,0:T(8,128)(2,1)}) %all-gather.10.cloned.1.call-update) | async-done | bytes 2097168 | tf_op jit(solution)/shard_map/all_gather | solution.py:176
  87.7 2.0 convolution_bitcast_fusion.7
  91.5 2.5 convolution_convert_fusion.13
  94.0 39.7 %all-gather.12.cloned.1.call-done = bf16[2,4096,128]{2,1,0:T(8,128)(2,1)} async-done(((bf16[2,1024,128]{2,1,0:T(8,128)(2,1)}), bf16[2,4096,128]{2,1,0:T(8,128)(2,1)}) %all-gather.12.cloned.1.call-update) | async-done | bytes 2097168 | tf_op jit(solution)/shard_map/all_gather | solution.py:177
  133.7 2.7 convolution_convert_fusion.12
  136.4 3.5 fusion.75
  139.9 143.7 %all-gather.8.cloned.1.call-done = bf16[2,4096,512]{2,1,0:T(8,128)(2,1)} async-done(((bf16[2,1024,512]{2,1,0:T(8,128)(2,1)}), bf16[2,4096,512]{2,1,0:T(8,128)(2,1)}) %all-gather.8.cloned.1.call-update) | async-done | bytes 8388624 | tf_op jit(solution)/shard_map/all_gather | solution.py:175
  283.6 4.5 slice_bitcast_fusion.6
  288.1 6.6 copy.18
  294.7 3.8 fusion.78
  304.1 2.0 fusion.134
  306.8 4.8 convolution_convert_fusion.4
  311.6 5.5 fusion.45
  317.1 115.8 %all-gather.14.cloned.1.call-done = bf16[2,512,4096]{2,1,0:T(8,128)(2,1)} async-done(((bf16[2,512,1024]{2,1,0:T(8,128)(2,1)}), bf16[2,512,4096]{2,1,0:T(8,128)(2,1)}) %all-gather.14.cloned.1.call-update) | async-done | bytes 8388624 | tf_op jit(solution)/shard_map/all_gather | solution.py:178
  432.9 6.1 fusion.6
  439.0 6.7 copy.28
  445.7 72.4 %all-reduce.9.cloned.1.call-done = (bf16[256,4096]{1,0:T(8,128)(2,1)}, bf16[256,4096]{1,0:T(8,128)(2,1)}) async-done(((bf16[256,4096]{1,0:T(8,128)(2,1)}, bf16[256,4096]{1,0:T(8,128)(2,1)}), (bf16[256,4096]{1,0:T(8,128)(2,1)}, bf16[256,4096]{1,0:T(8,128)(2,1)})) %all-reduce.9.cloned.1.call-update) | async-done | bytes 4194320 | tf_op jit(solution)/shard_map/psum | solution.py:245
  518.2 3.7 fusion.32
  529.6 2.1 fusion.84
  532.9 4.4 fusion.81
  542.1 2.2 fusion.70
  544.6 3.1 multiply_reduce_fusion
  547.7 2.0 fusion.105
  549.8 3.3 fusion.102
  553.1 2.8 convolution_convert_fusion.9
  555.9 2.8 fusion.135
  558.7 2.0 fusion.88
  560.7 3.6 fusion.37
  564.2 4.9 fusion.7
  569.9 61.3 %all-reduce.5.cloned.1.call-done = bf16[256,4096]{1,0:T(8,128)(2,1)} async-done(((bf16[256,4096]{1,0:T(8,128)(2,1)}), bf16[256,4096]{1,0:T(8,128)(2,1)}) %all-reduce.5.cloned.1.call-update) | async-done | bytes 2097168 | tf_op jit(solution)/shard_map/psum | solution.py:241
  631.2 4.8 fusion.95
  637.0 2.9 convolution_bitcast_fusion.1
  639.8 2.8 convolution_bitcast_fusion.5
  645.1 2.1 fusion.107
  647.1 3.8 convolution_add_fusion
  650.9 2.0 fusion.8
  654.6 59.5 %all-reduce.7.cloned.1.call-done = bf16[256,4096]{1,0:T(8,128)(2,1)} async-done(((bf16[256,4096]{1,0:T(8,128)(2,1)}), bf16[256,4096]{1,0:T(8,128)(2,1)}) %all-reduce.7.cloned.1.call-update) | async-done | bytes 2097168 | tf_op jit(solution)/shard_map/psum | solution.py:305
  714.1 3.1 fusion.33
  717.6 3.9 fusion.24
  721.5 4.6 fusion.98
  727.4 3.3 convolution_bitcast_fusion.3
  731.9 2.3 fusion.13
  737.4 3.9 fusion.15
  741.3 2.8 pad_maximum_fusion.3
  744.2 4.3 fusion.3
  748.4 2.7 convolution_bitcast_fusion
  751.3 3.3 fusion.2
  754.7 7.6 pad_maximum_fusion
  763.8 5.2 fusion.5
  769.0 3.3 fusion.4
  772.3 6.2 pad_maximum_fusion.1
  778.6 2.1 convert_element_type.480
  780.7 42.9 %reduce-scatter.9.cloned.1.call-done = bf16[2,1024,128]{2,1,0:T(8,128)(2,1)} async-done(((bf16[2,4096,128]{2,1,0:T(8,128)(2,1)}), bf16[2,1024,128]{2,1,0:T(8,128)(2,1)}) %reduce-scatter.9.cloned.1.call-update) | async-done | bytes 524304 | tf_op jit(solution)/shard_map/reduce_scatter | solution.py:320
  823.6 2.1 convert_element_type.482
  825.7 144.1 %reduce-scatter.5.cloned.1.call-done = bf16[2,1024,512]{2,1,0:T(8,128)(2,1)} async-done(((bf16[2,4096,512]{2,1,0:T(8,128)(2,1)}), bf16[2,1024,512]{2,1,0:T(8,128)(2,1)}) %reduce-scatter.5.cloned.1.call-update) | async-done | bytes 2097168 | tf_op jit(solution)/shard_map/reduce_scatter | solution.py:314
  969.8 4.2 convert_element_type.479
  974.0 143.3 %reduce-scatter.11.cloned.1.call-done = bf16[2,512,1024]{2,1,0:T(8,128)(2,1)} async-done(((bf16[2,512,4096]{2,1,0:T(8,128)(2,1)}), bf16[2,512,1024]{2,1,0:T(8,128)(2,1)}) %reduce-scatter.11.cloned.1.call-update) | async-done | bytes 2097168 | tf_op jit(solution)/shard_map/reduce_scatter | solution.py:323
  1117.3 4.1 convert_element_type.483
  (197 shorter events, 40.8 us)
Async XLA Ops:
  7.2 33.2 %all-gather.6.cloned.1.call-start = ((), (), s32[]{:S(2)}) async-start(), calls=%async_computation.4 | async-start | bytes 2359296 | tf_op jit(solution)/shard_map/all_gather | solution.py:189
  7.9 79.8 %all-gather.10.cloned.1.call-start = ((), (), s32[]{:S(2)}) async-start(), calls=%async_computation.6 | async-start | bytes 2621440 | tf_op jit(solution)/shard_map/all_gather | solution.py:176
  8.6 125.1 %all-gather.12.cloned.1.call-start = ((), (), s32[]{:S(2)}) async-start(), calls=%async_computation.7 | async-start | bytes 2621440 | tf_op jit(solution)/shard_map/all_gather | solution.py:177
  9.4 274.2 %all-gather.8.cloned.1.call-start = ((), (), s32[]{:S(2)}) async-start(), calls=%async_computation.5 | async-start | bytes 10485760 | tf_op jit(solution)/shard_map/all_gather | solution.py:175
  10.0 422.9 %all-gather.14.cloned.1.call-start = ((), (), s32[]{:S(2)}) async-start(), calls=%async_computation.8 | async-start | bytes 10485760 | tf_op jit(solution)/shard_map/all_gather | solution.py:178
  10.5 507.6 %all-reduce.9.cloned.1.call-start = ((), (), s32[]{:S(2)}) async-start(), calls=%async_computation.15 | async-start | bytes 8388608 | tf_op jit(solution)/shard_map/psum | solution.py:245
  16.4 6.4 copy-start.56
  16.4 8.7 copy-start.42
  23.4 66.4 %copy-start.47 = (f32[64]{0:T(128)}, f32[64]{0:T(128)S(1)}, u32[]{:S(2)}) copy-start(f32[64]{0:T(128)S(1)} %multiply_exponential_fusion) | copy-start | bytes 772
  24.1 65.7 %copy-start.43 = (f32[256]{0:T(256)}, f32[256]{0:T(256)S(1)}, u32[]{:S(2)}) copy-start(f32[256]{0:T(256)S(1)} %iota_convert_fusion) | copy-start | bytes 3076
  44.7 250.0 %copy-start = (bf16[256,4096]{1,0:T(8,128)(2,1)}, bf16[256,4096]{1,0:T(8,128)(2,1)S(1)}, u32[]{:S(2)}) copy-start(bf16[256,4096]{1,0:T(8,128)(2,1)S(1)} %fusion.28) | copy-start | bytes 6291460
  298.6 1.9 copy-start.33
  298.6 2.3 copy-start.38
  298.7 7.3 copy-start.23
  298.8 7.3 copy-start.24
  298.8 3.5 copy-start.30
  302.5 3.6 copy-start.37
  439.0 192.2 %all-reduce.5.cloned.1.call-start = ((), (), s32[]{:S(2)}) async-start(), calls=%async_computation.9 | async-start | bytes 4194304 | tf_op jit(solution)/shard_map/psum | solution.py:241
  439.0 79.1 %copy-start.7 = (bf16[256,4096]{1,0:T(8,128)(2,1)S(1)}, bf16[256,4096]{1,0:T(8,128)(2,1)}, u32[]{:S(2)}) copy-start(bf16[256,4096]{1,0:T(8,128)(2,1)} %all-gather.6.cloned.1.call-done) | copy-start | bytes 6291460
  518.2 3.8 copy-start.2
  518.2 8.4 slice-start.2
  521.9 1.9 copy-start.5
  521.9 1.9 copy-start.51
  522.0 2.3 copy-start.11
  522.0 3.3 copy-start.16
  522.0 5.0 slice-start.3
  523.8 4.5 copy-start.8
  524.3 4.0 slice-start
  527.0 2.6 slice-start.1
  532.9 4.5 copy-start.18
  532.9 5.3 copy-start.9
  532.9 5.3 copy-start.12
  540.2 4.1 copy-start.31
  541.4 2.9 copy-start.25
  541.4 2.9 copy-start.26
  560.7 3.6 copy-start.20
  569.2 144.9 %all-reduce.7.cloned.1.call-start = ((), (), s32[]{:S(2)}) async-start(), calls=%async_computation.10 | async-start | bytes 4194304 | tf_op jit(solution)/shard_map/psum | solution.py:305
  569.9 61.3 %copy-start.53 = (f32[256]{0:T(256)}, f32[256]{0:T(256)S(1)}, u32[]{:S(2)}) copy-start(f32[256]{0:T(256)S(1)} %compare_convert_fusion) | copy-start | bytes 3076
  631.2 5.5 copy-start.41
  642.6 1.9 copy-start.36
  642.6 2.0 copy-start.45
  642.6 2.0 copy-start.49
  642.6 2.3 copy-start.22
  644.6 6.3 copy-start.29
  644.9 6.0 copy-start.27
  644.9 6.0 copy-start.28
  645.0 5.9 copy-start.15
  647.1 3.8 copy-start.17
  653.0 125.6 %reduce-scatter.7.cloned.1.call-start = ((), (), s32[]{:S(2)}) async-start(), calls=%async_computation.12 | async-start | bytes 2621440 | tf_op jit(solution)/shard_map/reduce_scatter | solution.py:317
  714.1 3.2 copy-start.3
  714.1 3.5 copy-start.6
  714.1 3.5 copy-start.52
  714.1 3.5 copy-start.54
  721.5 4.6 copy-start.13
  721.5 4.6 copy-start.40
  721.5 9.2 copy-start.46
  721.5 9.2 copy-start.50
  735.8 87.9 %reduce-scatter.9.cloned.1.call-start = ((), (), s32[]{:S(2)}) async-start(), calls=%async_computation.13 | async-start | bytes 2621440 | tf_op jit(solution)/shard_map/reduce_scatter | solution.py:320
  744.1 4.3 copy-start.34
  744.1 225.7 %reduce-scatter.5.cloned.1.call-start = ((), (), s32[]{:S(2)}) async-start(), calls=%async_computation.11 | async-start | bytes 10485760 | tf_op jit(solution)/shard_map/reduce_scatter | solution.py:314
  748.4 2.9 copy-start.1
  762.3 355.1 %reduce-scatter.11.cloned.1.call-start = ((), (), s32[]{:S(2)}) async-start(), calls=%async_computation.14 | async-start | bytes 10485760 | tf_op jit(solution)/shard_map/reduce_scatter | solution.py:323
  763.8 5.2 copy-start.14
  769.0 3.3 copy-start.10
  (9 other events, 12.7 us)
Sparse Core Ops, SparseCore 0:
  9.9 30.4 all-gather.5
  42.0 45.6 all-gather.9
  89.3 44.4 all-gather.11
  135.2 148.4 all-gather.7
  285.0 147.7 all-gather.13
  439.1 79.0 all-reduce.8
  569.3 61.8 all-reduce.4
  653.1 60.9 all-reduce.6
  735.9 42.6 reduce-scatter.6
  780.8 42.8 reduce-scatter.8
  826.0 143.7 reduce-scatter.4
  972.1 145.2 reduce-scatter.10
where the time goes:
time: 1140 us; the launch traced here: 1130 us
  waiting for transfers between devices  881 us (77%)
  matrix products  138 us (12%)
  other arithmetic  54.1 us (5%)
  local copies, waits for them, and re-layouts  38.4 us (3%)
  between operations  15.4 us (1%)
    reduce_scatter x1, waiting for transfers between devices, body(): lax.psum_scatter(query_stack.astype(jnp.bfloat16), 'dp', scatter_dimensio...  144 us
    all_gather x1, waiting for transfers between devices, body(): lax.all_gather(query_probe, 'dp', axis=1, tiled=True)  144 us
    reduce_scatter x1, waiting for transfers between devices, body(): lax.psum_scatter(out_stack.astype(jnp.bfloat16), 'dp', scatter_dimension=...  143 us
    all_gather x1, waiting for transfers between devices, body(): lax.all_gather(out_probe, 'dp', axis=2, tiled=True)  116 us
    psum x1, waiting for transfers between devices, body(): lax.psum(primal_part.astype(jnp.bfloat16), 'tensor').astype(jnp.float32)  72.4 us
    psum x1, waiting for transfers between devices, body(): lax.psum(tangent_part.astype(jnp.bfloat16), 'tensor').astype(jnp.float32)  61.3 us
    psum x1, waiting for transfers between devices, body(): lax.psum(grad_part.astype(jnp.bfloat16), 'tensor').astype(jnp.float32)  59.5 us
    dot_general x20, matrix products, matmul(): return jnp.dot(left_side, right_side, preferred_element_type=jnp.float32)  59.3 us
  transfers between devices with their start and end apart: 12, of which 12 were waited for; matrix products, arithmetic and copies ran while one was open for 11% of the time, Pallas kernels for 0%

commit v1 on v0

--- a/solution.py
+++ b/solution.py
@@ -9,6 +9,12 @@
 LEN = 256
 EPS = 1e-05
 THETA = 500000.0
+
+
+def summed_here(block, axis):
+    pieces = lax.all_gather(block, axis, axis=0, tiled=False)
+    total = pieces.sum(axis=0)
+    return total
 
 
 def swapped(value, axis, apart):
@@ -242,7 +248,7 @@
         else:
             primal_part = matmul(blended, out_weight[layer_index])
             primal_sum, tangent_sum = (
-                lax.psum(primal_part.astype(jnp.bfloat16), "tensor").astype(jnp.float32),
+                summed_here(primal_part.astype(jnp.bfloat16), "tensor").astype(jnp.float32),
                 lax.psum(tangent_part.astype(jnp.bfloat16), "tensor").astype(jnp.float32),
             )
         stored.append((wide_stream, inverse, normed_all, queries, key_heads, value_heads, blended))

time: 1140 us -> 1210 us (1.061)
  waiting for transfers between devices: 881 us -> 937 us
  other arithmetic: 54.1 us -> 69.8 us
    all_gather x0 -> x1, waiting for transfers between devices: none -> 76.8 us  [summed_here(): pieces = lax.all_gather(block, axis, axis=0, tiled=False)]
    psum x1 -> x0, waiting for transfers between devices: 72.4 us -> none  [body(): lax.psum(primal_part.astype(jnp.bfloat16), 'tensor').astype(jnp.float32)]
    psum x1 -> x2, waiting for transfers between devices: 61.3 us -> 114 us  [body(): lax.psum(tangent_part.astype(jnp.bfloat16), 'tensor').astype(jnp.float32)]
    reduce_scatter x1, waiting for transfers between devices: 42.9 us -> 0.02 us  [body(): lax.psum_scatter(value_stack.astype(jnp.bfloat16), 'dp', scatter_dimensio...]
    reduce_scatter x1, waiting for transfers between devices: 0.08 us -> 38.6 us  [body(): lax.psum_scatter(key_stack.astype(jnp.bfloat16), 'dp', scatter_dimension=...]
    all_gather x1, waiting for transfers between devices: 116 us -> 136 us  [body(): lax.all_gather(out_probe, 'dp', axis=2, tiled=True)]
    all_gather x1, waiting for transfers between devices: 39.7 us -> 23 us  [body(): lax.all_gather(value_probe, 'dp', axis=1, tiled=True)]
  transfers between devices with their start and end apart: 12 -> 13, of which waited for: 12 -> 12; matrix products, arithmetic and copies ran while one was open for 11% -> 12% of each run, Pallas kernels for 0% -> 0%
where the time goes in v1:
time: 1210 us; the launch traced here: 1200 us
  waiting for transfers between devices  937 us (77%)
  matrix products  138 us (11%)
  other arithmetic  69.8 us (6%)
  local copies, waits for them, and re-layouts  36.6 us (3%)
  between operations  15 us (1%)
    reduce_scatter x1, waiting for transfers between devices, body(): lax.psum_scatter(out_stack.astype(jnp.bfloat16), 'dp', scatter_dimension=...  144 us
    reduce_scatter x1, waiting for transfers between devices, body(): lax.psum_scatter(query_stack.astype(jnp.bfloat16), 'dp', scatter_dimensio...  144 us
    all_gather x1, waiting for transfers between devices, body(): lax.all_gather(query_probe, 'dp', axis=1, tiled=True)  142 us
    all_gather x1, waiting for transfers between devices, body(): lax.all_gather(out_probe, 'dp', axis=2, tiled=True)  136 us
    psum x2, waiting for transfers between devices, body(): lax.psum(tangent_part.astype(jnp.bfloat16), 'tensor').astype(jnp.float32)  114 us
    all_gather x1, waiting for transfers between devices, summed_here(): pieces = lax.all_gather(block, axis, axis=0, tiled=False)  76.8 us
    psum x1, waiting for transfers between devices, body(): lax.psum(grad_part.astype(jnp.bfloat16), 'tensor').astype(jnp.float32)  59.3 us
    dot_general x20, matrix products, matmul(): return jnp.dot(left_side, right_side, preferred_element_type=jnp.float32)  54.6 us
  transfers between devices with their start and end apart: 13, of which 12 were waited for; matrix products, arithmetic and copies ran while one was open for 12% of the time, Pallas kernels for 0%

profile of v1, /device:TPU:0, one launch (start us, length us, event | category | flops | bytes accessed | tf_op | source)
XLA Modules:
  0.0 1196.5 jit_solution(4215428419927240356)
XLA Ops:
  10.6 5.8 slice_bitcast_fusion.8
  16.4 6.4 copy.15
  25.2 15.2 %all-gather.8.cloned.1.call-done = bf16[256,4096]{1,0:T(8,128)(2,1)} async-done(((bf16[32,4096]{1,0:T(8,128)(2,1)}), bf16[256,4096]{1,0:T(8,128)(2,1)}) %all-gather.8.cloned.1.call-update) | async-done | bytes 2097168 | tf_op jit(solution)/shard_map/all_gather | solution.py:195
  40.4 2.1 fusion.26
  42.5 2.2 fusion.28
  44.7 2.8 convolution_bitcast_fusion.8
  47.5 40.2 %all-gather.12.cloned.1.call-done = bf16[2,4096,128]{2,1,0:T(8,128)(2,1)} async-done(((bf16[2,1024,128]{2,1,0:T(8,128)(2,1)}), bf16[2,4096,128]{2,1,0:T(8,128)(2,1)}) %all-gather.12.cloned.1.call-update) | async-done | bytes 2097168 | tf_op jit(solution)/shard_map/all_gather | solution.py:182
  87.7 2.2 convolution_bitcast_fusion.7
  91.5 2.5 convolution_convert_fusion.13
  95.4 142.3 %all-gather.10.cloned.1.call-done = bf16[2,4096,512]{2,1,0:T(8,128)(2,1)} async-done(((bf16[2,1024,512]{2,1,0:T(8,128)(2,1)}), bf16[2,4096,512]{2,1,0:T(8,128)(2,1)}) %all-gather.10.cloned.1.call-update) | async-done | bytes 8388624 | tf_op jit(solution)/shard_map/all_gather | solution.py:181
  237.7 4.5 slice_bitcast_fusion.6
  242.2 6.4 copy.18
  248.6 3.5 fusion.78
  254.7 4.8 convolution_convert_fusion.4
  260.0 23.0 %all-gather.14.cloned.1.call-done = bf16[2,4096,128]{2,1,0:T(8,128)(2,1)} async-done(((bf16[2,1024,128]{2,1,0:T(8,128)(2,1)}), bf16[2,4096,128]{2,1,0:T(8,128)(2,1)}) %all-gather.14.cloned.1.call-update) | async-done | bytes 2097168 | tf_op jit(solution)/shard_map/all_gather | solution.py:183
  283.0 2.0 convolution_convert_fusion.12
  290.7 6.1 fusion.45
  296.8 136.1 %all-gather.16.cloned.1.call-done = bf16[2,512,4096]{2,1,0:T(8,128)(2,1)} async-done(((bf16[2,512,1024]{2,1,0:T(8,128)(2,1)}), bf16[2,512,4096]{2,1,0:T(8,128)(2,1)}) %all-gather.16.cloned.1.call-update) | async-done | bytes 8388624 | tf_op jit(solution)/shard_map/all_gather | solution.py:184
  432.9 6.1 fusion.6
  439.0 6.7 copy.28
  445.8 76.8 %all-gather.18.cloned.1.call-done = bf16[2048,4096]{1,0:T(8,128)(2,1)} async-done(((bf16[256,4096]{1,0:T(8,128)(2,1)}), bf16[2048,4096]{1,0:T(8,128)(2,1)}) %all-gather.18.cloned.1.call-update) | async-done | bytes 16777232 | tf_op jit(solution)/shard_map/all_gather | solution.py:15
  522.5 10.8 reduce_sum.141
  533.4 54.2 %all-reduce.4.cloned.1.call-done = bf16[256,4096]{1,0:T(8,128)(2,1)} async-done(((bf16[256,4096]{1,0:T(8,128)(2,1)}), bf16[256,4096]{1,0:T(8,128)(2,1)}) %all-reduce.4.cloned.1.call-update) | async-done | bytes 2097168 | tf_op jit(solution)/shard_map/psum | solution.py:252
  587.6 3.7 fusion.32
  596.5 2.1 fusion.81
  602.6 2.1 fusion.84
  608.8 2.3 fusion.70
  611.1 2.3 convolution_convert_fusion.9
  613.3 2.1 fusion.105
  615.4 3.3 fusion.102
  622.0 3.5 multiply_reduce_fusion
  625.5 2.7 fusion.135
  630.2 3.6 fusion.37
  633.8 4.9 fusion.7
  639.5 60.3 %all-reduce.6.cloned.1.call-done = bf16[256,4096]{1,0:T(8,128)(2,1)} async-done(((bf16[256,4096]{1,0:T(8,128)(2,1)}), bf16[256,4096]{1,0:T(8,128)(2,1)}) %all-reduce.6.cloned.1.call-update) | async-done | bytes 2097168 | tf_op jit(solution)/shard_map/psum | solution.py:247
  699.7 4.8 fusion.95
  705.2 2.2 fusion.103
  708.7 2.7 convolution_bitcast_fusion.5
  711.4 2.8 convolution_bitcast_fusion.1
  717.6 3.8 convolution_add_fusion
  721.4 2.0 fusion.8
  725.1 59.3 %all-reduce.8.cloned.1.call-done = bf16[256,4096]{1,0:T(8,128)(2,1)} async-done(((bf16[256,4096]{1,0:T(8,128)(2,1)}), bf16[256,4096]{1,0:T(8,128)(2,1)}) %all-reduce.8.cloned.1.call-update) | async-done | bytes 2097168 | tf_op jit(solution)/shard_map/psum | solution.py:311
  784.5 3.1 fusion.33
  787.9 3.9 fusion.24
  791.8 5.3 fusion.98
  797.1 3.9 fusion.15
  801.0 2.8 pad_maximum_fusion.3
  805.4 2.2 fusion.148
  807.6 3.7 convolution_bitcast_fusion.3
  812.5 2.3 fusion.13
  816.5 5.8 fusion.5
  822.3 3.3 fusion.4
  825.6 7.6 pad_maximum_fusion.1
  834.1 3.3 fusion.3
  837.4 2.8 convolution_bitcast_fusion
  840.3 3.3 fusion.2
  843.6 7.5 pad_maximum_fusion
  851.2 2.1 convert_element_type.484
  853.3 38.6 %reduce-scatter.7.cloned.1.call-done = bf16[2,1024,128]{2,1,0:T(8,128)(2,1)} async-done(((bf16[2,4096,128]{2,1,0:T(8,128)(2,1)}), bf16[2,1024,128]{2,1,0:T(8,128)(2,1)}) %reduce-scatter.7.cloned.1.call-update) | async-done | bytes 524304 | tf_op jit(solution)/shard_map/reduce_scatter | solution.py:323
  891.8 2.1 convert_element_type.482
  893.9 144.0 %reduce-scatter.11.cloned.1.call-done = bf16[2,512,1024]{2,1,0:T(8,128)(2,1)} async-done(((bf16[2,512,4096]{2,1,0:T(8,128)(2,1)}), bf16[2,512,1024]{2,1,0:T(8,128)(2,1)}) %reduce-scatter.11.cloned.1.call-update) | async-done | bytes 2097168 | tf_op jit(solution)/shard_map/reduce_scatter | solution.py:329
  1037.9 4.1 convert_element_type.485
  1042.0 143.6 %reduce-scatter.5.cloned.1.call-done = bf16[2,1024,512]{2,1,0:T(8,128)(2,1)} async-done(((bf16[2,4096,512]{2,1,0:T(8,128)(2,1)}), bf16[2,1024,512]{2,1,0:T(8,128)(2,1)}) %reduce-scatter.5.cloned.1.call-update) | async-done | bytes 2097168 | tf_op jit(solution)/shard_map/reduce_scatter | solution.py:320
  1185.5 4.2 convert_element_type.481
  (199 shorter events, 48.9 us)
Async XLA Ops:
  7.2 33.2 %all-gather.8.cloned.1.call-start = ((), (), s32[]{:S(2)}) async-start(), calls=%async_computation.4 | async-start | bytes 2359296 | tf_op jit(solution)/shard_map/all_gather | solution.py:195
  7.9 79.8 %all-gather.12.cloned.1.call-start = ((), (), s32[]{:S(2)}) async-start(), calls=%async_computation.6 | async-start | bytes 2621440 | tf_op jit(solution)/shard_map/all_gather | solution.py:182
  8.6 229.0 %all-gather.10.cloned.1.call-start = ((), (), s32[]{:S(2)}) async-start(), calls=%async_computation.5 | async-start | bytes 10485760 | tf_op jit(solution)/shard_map/all_gather | solution.py:181
  9.4 273.6 %all-gather.14.cloned.1.call-start = ((), (), s32[]{:S(2)}) async-start(), calls=%async_computation.7 | async-start | bytes 2621440 | tf_op jit(solution)/shard_map/all_gather | solution.py:183
  10.0 422.9 %all-gather.16.cloned.1.call-start = ((), (), s32[]{:S(2)}) async-start(), calls=%async_computation.8 | async-start | bytes 10485760 | tf_op jit(solution)/shard_map/all_gather | solution.py:184
  10.5 512.0 %all-gather.18.cloned.1.call-start = ((), (), s32[]{:S(2)}) async-start(), calls=%async_computation.16 | async-start | bytes 18874368 | tf_op jit(solution)/shard_map/all_gather | solution.py:15
  16.4 6.4 copy-start.55
  16.4 8.7 copy-start.43
  23.5 66.4 %copy-start.47 = (f32[64]{0:T(128)}, f32[64]{0:T(128)S(1)}, u32[]{:S(2)}) copy-start(f32[64]{0:T(128)S(1)} %multiply_exponential_fusion) | copy-start | bytes 772
  24.1 65.8 %copy-start.44 = (f32[256]{0:T(256)}, f32[256]{0:T(256)S(1)}, u32[]{:S(2)}) copy-start(f32[256]{0:T(256)S(1)} %iota_convert_fusion) | copy-start | bytes 3076
  44.7 238.3 %copy-start = (bf16[256,4096]{1,0:T(8,128)(2,1)}, bf16[256,4096]{1,0:T(8,128)(2,1)S(1)}, u32[]{:S(2)}) copy-start(bf16[256,4096]{1,0:T(8,128)(2,1)S(1)} %fusion.28) | copy-start | bytes 6291460
  87.7 6.4 copy-start.11
  254.7 5.1 copy-start.37
  254.7 5.1 copy-start.38
  259.6 25.5 %copy-start.26 = (bf16[256,4,64]{0,2,1:T(8,128)(2,1)S(1)}, bf16[256,4,64]{0,2,1:T(8,128)(2,1)}, u32[]{:S(2)}) copy-start(bf16[256,4,64]{0,2,1:T(8,128)(2,1)} %get-tuple-element.142) | copy-start | bytes 393220
  259.6 25.5 %copy-start.27 = (bf16[256,4,64]{0,2,1:T(8,128)(2,1)S(1)}, bf16[256,4,64]{0,2,1:T(8,128)(2,1)}, u32[]{:S(2)}) copy-start(bf16[256,4,64]{0,2,1:T(8,128)(2,1)} %get-tuple-element.152) | copy-start | bytes 393220
  259.6 25.5 %copy-start.33 = (bf16[256,128]{0,1:T(8,128)(2,1)S(1)}, bf16[256,128]{0,1:T(8,128)(2,1)}, u32[]{:S(2)}) copy-start(bf16[256,128]{0,1:T(8,128)(2,1)} %pad_maximum_fusion.7) | copy-start | bytes 196612
  259.6 25.9 %copy-start.20 = (bf16[256,4,64]{0,2,1:T(8,128)(2,1)S(1)}, bf16[256,4,64]{0,2,1:T(8,128)(2,1)}, u32[]{:S(2)}) copy-start(bf16[256,4,64]{0,2,1:T(8,128)(2,1)} %get-tuple-element.106) | copy-start | bytes 393220
  259.6 25.9 %copy-start.21 = (bf16[256,4,64]{0,2,1:T(8,128)(2,1)S(1)}, bf16[256,4,64]{0,2,1:T(8,128)(2,1)}, u32[]{:S(2)}) copy-start(bf16[256,4,64]{0,2,1:T(8,128)(2,1)} %get-tuple-element.116) | copy-start | bytes 393220
  259.6 25.9 %copy-start.41 = (pred[256,256]{0,1:T(8,128)(4,1)S(1)}, pred[256,256]{0,1:T(8,128)(4,1)}, u32[]{:S(2)}) copy-start(pred[256,256]{0,1:T(8,128)(4,1)} %fusion.161) | copy-start | bytes 196612
  259.6 327.9 %all-reduce.4.cloned.1.call-start = ((), (), s32[]{:S(2)}) async-start(), calls=%async_computation.9 | async-start | bytes 4194304 | tf_op jit(solution)/shard_map/psum | solution.py:252
  439.0 260.8 %all-reduce.6.cloned.1.call-start = ((), (), s32[]{:S(2)}) async-start(), calls=%async_computation.10 | async-start | bytes 4194304 | tf_op jit(solution)/shard_map/psum | solution.py:247
  522.5 65.0 %copy-start.6 = (bf16[256,4096]{1,0:T(8,128)(2,1)S(1)}, bf16[256,4096]{1,0:T(8,128)(2,1)}, u32[]{:S(2)}) copy-start(bf16[256,4096]{1,0:T(8,128)(2,1)} %all-gather.8.cloned.1.call-done) | copy-start | bytes 6291460
  587.6 3.8 copy-start.2
  587.6 12.7 %slice-start.2 = ((s8[8388608]{0:T(1024)(128)(4,1)}), s8[4194304]{0:T(1024)(128)(4,1)S(1)}, s32[]{:S(2)}) async-start(s8[8388608]{0:T(1024)(128)(4,1)} %bitcast.274), calls=%async_computation.19 | async-start | bytes 8388608
  591.4 2.3 copy-start.8
  591.4 3.3 copy-start.15
  593.2 8.4 copy-start.7
  593.2 3.3 copy-start.12
  593.7 6.6 slice-start.3
  596.0 2.6 copy-start.17
  598.6 3.0 slice-start
  602.6 3.4 copy-start.45
  602.6 3.4 copy-start.48
  606.9 8.5 copy-start.35
  608.8 6.6 copy-start.22
  608.8 6.6 copy-start.24
  613.3 5.5 copy-start.39
  613.3 5.5 copy-start.40
  613.3 6.2 copy-start.28
  630.2 3.6 copy-start.18
  638.8 145.7 %all-reduce.8.cloned.1.call-start = ((), (), s32[]{:S(2)}) async-start(), calls=%async_computation.11 | async-start | bytes 4194304 | tf_op jit(solution)/shard_map/psum | solution.py:311
  639.4 65.1 %copy-start.52 = (f32[256]{0:T(256)}, f32[256]{0:T(256)S(1)}, u32[]{:S(2)}) copy-start(f32[256]{0:T(256)S(1)} %compare_convert_fusion) | copy-start | bytes 3076
  639.4 65.8 %copy-start.23 = (bf16[256,4,64]{0,2,1:T(8,128)(2,1)S(1)}, bf16[256,4,64]{0,2,1:T(8,128)(2,1)}, u32[]{:S(2)}) copy-start(bf16[256,4,64]{0,2,1:T(8,128)(2,1)} %copy-done.22) | copy-start | bytes 393220
  639.4 65.8 %copy-start.25 = (bf16[256,4,64]{0,2,1:T(8,128)(2,1)S(1)}, bf16[256,4,64]{0,2,1:T(8,128)(2,1)}, u32[]{:S(2)}) copy-start(bf16[256,4,64]{0,2,1:T(8,128)(2,1)} %copy-done.24) | copy-start | bytes 393220
  639.5 65.8 %copy-start.36 = (bf16[256,128]{0,1:T(8,128)(2,1)S(1)}, bf16[256,128]{0,1:T(8,128)(2,1)}, u32[]{:S(2)}) copy-start(bf16[256,128]{0,1:T(8,128)(2,1)} %copy-done.35) | copy-start | bytes 196612
  714.2 3.3 copy-start.19
  717.6 3.8 copy-start.13
  717.6 3.8 copy-start.16
  717.6 3.8 copy-start.31
  723.5 127.7 %reduce-scatter.9.cloned.1.call-start = ((), (), s32[]{:S(2)}) async-start(), calls=%async_computation.14 | async-start | bytes 2621440 | tf_op jit(solution)/shard_map/reduce_scatter | solution.py:326
  784.5 3.2 copy-start.3
  784.5 3.5 copy-start.5
  784.5 3.5 copy-start.51
  784.5 3.5 copy-start.53
  791.8 5.3 copy-start.9
  803.8 7.5 copy-start.46
  803.8 7.5 copy-start.49
  803.8 88.0 %reduce-scatter.7.cloned.1.call-start = ((), (), s32[]{:S(2)}) async-start(), calls=%async_computation.13 | async-start | bytes 2621440 | tf_op jit(solution)/shard_map/reduce_scatter | solution.py:323
  816.4 221.5 %reduce-scatter.11.cloned.1.call-start = ((), (), s32[]{:S(2)}) async-start(), calls=%async_computation.15 | async-start | bytes 10485760 | tf_op jit(solution)/shard_map/reduce_scatter | solution.py:329
  816.4 5.9 copy-start.10
  833.2 4.3 copy-start.34
  833.2 352.3 %reduce-scatter.5.cloned.1.call-start = ((), (), s32[]{:S(2)}) async-start(), calls=%async_computation.12 | async-start | bytes 10485760 | tf_op jit(solution)/shard_map/reduce_scatter | solution.py:320
  837.4 2.9 copy-start.1
  (9 other events, 15.1 us)
Sparse Core Ops, SparseCore 0:
  9.9 30.4 all-gather.7
  42.0 45.6 all-gather.11
  89.3 148.3 all-gather.9
  239.1 43.8 all-gather.13
  284.4 148.4 all-gather.15
  434.6 87.9 all-gather.17
  525.8 61.7 all-reduce.3
  638.9 60.8 all-reduce.5
  723.6 60.8 all-reduce.7
  803.9 42.6 reduce-scatter.8
  849.0 42.8 reduce-scatter.6
  894.0 143.7 reduce-scatter.10
  1040.2 145.2 reduce-scatter.4
